TPU v7x, 32 devices: a whole 2x2x4 slice. The times are simulated.
32 devices in a mesh: groups: 2 (over y), ctx: 16 (over z, x, core).
Axes of the slice: x: 2, y: 2, z: 4, core: 2. Of those that a mesh axis runs over, the one named last changes fastest.
Arguments:
- prompt_query: bfloat16 [2048, 4096], P(('groups', 'ctx')), parts along dimension 0, may hold values from -6 to 6
- prompt_key: bfloat16 [2048, 512], P(('groups', 'ctx')), parts along dimension 0, may hold values from -6 to 6
- prompt_value: bfloat16 [2048, 512], P(('groups', 'ctx')), parts along dimension 0, may hold values from -6 to 6
- prefix_key_cache: bfloat16 [256, 512], P(('groups', 'ctx')), parts along dimension 0, may hold values from -6 to 6
- prefix_value_cache: bfloat16 [256, 512], P(('groups', 'ctx')), parts along dimension 0, may hold values from -6 to 6
- decoded_query: bfloat16 [8192], P('groups'), parts along dimension 0, may hold values from -6 to 6
- decoded_key: bfloat16 [1024], P('groups'), parts along dimension 0, may hold values from -6 to 6
- decoded_value: bfloat16 [1024], P('groups'), parts along dimension 0, may hold values from -6 to 6
- shard_counts: int32 [32, 2], P('groups'), parts along dimension 0, may hold values from 0 to 32, as said below
- block_offsets: int32 [32, 2], P('groups'), parts along dimension 0, may hold values from 0 to 992, as said below
Outputs:
- span_out: bfloat16 [2048, 4096], P(('groups', 'ctx')), parts along dimension 0
- next_out: bfloat16 [8192], P('groups'), parts along dimension 0
There are 2 independent parts, one for each index of `groups`. A program takes and returns all parts, laid end to end along the dimension named above; each array names one. Nothing has to cross between parts.
Inputs may be any that keep to these rules, and one draw needn't show every extreme that they name: block_offsets[i, 0] = 32 * p_i and block_offsets[i, 1] = 32 * (31 - p_i) for a permutation p of 0 to 15. shard_counts[i, h] = min(32, max(0, L - block_offsets[i, h])) for one prompt length L with 512 < L <= 960.
All inputs are finite; a program needn't handle non-finite values.
Results may differ from a plain program's by a relative error of at most 0.0055.
Values may be sent and summed in bfloat16 or wider, within the bound.
A program may use at most 128 MiB of HBM per device.

v0:
```python
import jax
import jax.numpy as jnp
from jax import lax
from jax.sharding import PartitionSpec as P

QUERY_HEADS = 32
KEY_VALUE_HEADS = 4
HEAD_WIDTH = 128
HEADS_PER_GROUP = 8


NEGATIVE_FILL = -1e30


def slot_lookup(lookup, shard_ids, devices):
    picked = shard_ids[:, None] == jnp.arange(devices, dtype=jnp.int32)[None, :]
    first_col = jnp.sum(jnp.where(picked, lookup[None, :, 0], 0), axis=1)
    second = jnp.sum(jnp.where(picked, lookup[None, :, 1], 0), axis=1)
    return (first_col, second)


def key_layout(row_ids, prior_rows, span_rows, prior_total, devices, shard_counts, block_offsets):
    per_shard = prior_rows + span_rows
    shard_ids = row_ids // per_shard
    within = row_ids % per_shard
    half_rows = span_rows // 2
    local_rows = within - prior_rows
    second = local_rows >= half_rows
    offset_in = jnp.where(second, local_rows - half_rows, local_rows)
    offset_first, offset_second = slot_lookup(block_offsets, shard_ids, devices)
    count_first, count_second = slot_lookup(shard_counts, shard_ids, devices)
    position = prior_total + jnp.where(second, offset_second, offset_first) + offset_in
    is_live = offset_in < jnp.where(second, count_second, count_first)
    in_prior = within < prior_rows
    return (jnp.where(in_prior, shard_ids * prior_rows + within, position), in_prior | is_live)


def body(
    prompt_query,
    prompt_key,
    prompt_value,
    prefix_key_cache,
    prefix_value_cache,
    decoded_query,
    decoded_key,
    decoded_value,
    shard_counts,
    block_offsets,
):
    devices = lax.axis_size("ctx")
    position_now = lax.axis_index("ctx")
    prompt_slot_count = prompt_query.shape[0]
    half_rows = prompt_slot_count // 2
    prior_rows = prefix_key_cache.shape[0]
    prior_total = prior_rows * devices
    logit_scale = HEAD_WIDTH ** (-0.5)
    own_offsets = lax.dynamic_slice_in_dim(block_offsets, position_now, 1, 0)[0]
    own_counts = lax.dynamic_slice_in_dim(shard_counts, position_now, 1, 0)[0]
    slot_ids = jnp.arange(prompt_slot_count, dtype=jnp.int32)
    second = slot_ids >= half_rows
    offset_in = jnp.where(second, slot_ids - half_rows, slot_ids)
    query_pos = prior_total + jnp.where(second, own_offsets[1], own_offsets[0]) + offset_in
    query_live = offset_in < jnp.where(second, own_counts[1], own_counts[0])
    query_head_list = prompt_query.reshape(
        prompt_slot_count, KEY_VALUE_HEADS, HEADS_PER_GROUP, HEAD_WIDTH
    )

    def update(state_now, head_key_rows, head_value_rows, key_pos, key_live):
        visible = key_live[None, :] & (key_pos[None, :] <= query_pos[:, None])
        peaks, totals, value_mixture = state_now
        total_row_count = head_key_rows.shape[0]
        scores = (
            jnp.einsum(
                "tgqd,rgd->tgqr",
                query_head_list,
                head_key_rows.reshape(total_row_count, KEY_VALUE_HEADS, HEAD_WIDTH),
                preferred_element_type=jnp.float32,
            )
            * logit_scale
        )
        seen = visible[:, None, None, :]
        scores = jnp.where(seen, scores, NEGATIVE_FILL)
        new_peaks = jnp.maximum(peaks, jnp.max(scores, axis=-1))
        weights = jnp.where(seen, jnp.exp(scores - new_peaks[..., None]), 0.0)
        rescale = jnp.exp(peaks - new_peaks)
        summed = jnp.einsum(
            "tgqr,rgd->tgqd",
            weights.astype(jnp.bfloat16),
            head_value_rows.reshape(total_row_count, KEY_VALUE_HEADS, HEAD_WIDTH),
            preferred_element_type=jnp.float32,
        )
        return (
            new_peaks,
            rescale * totals + jnp.sum(weights, axis=-1),
            rescale[..., None] * value_mixture + summed,
        )

    initial = (
        jnp.full((prompt_slot_count, KEY_VALUE_HEADS, HEADS_PER_GROUP), NEGATIVE_FILL, jnp.float32),
        jnp.zeros((prompt_slot_count, KEY_VALUE_HEADS, HEADS_PER_GROUP), jnp.float32),
        jnp.zeros((prompt_slot_count, KEY_VALUE_HEADS, HEADS_PER_GROUP, HEAD_WIDTH), jnp.float32),
    )
    joined_key_rows = jnp.concatenate([prefix_key_cache, prompt_key], 0)
    joined_value_rows = jnp.concatenate([prefix_value_cache, prompt_value], 0)
    pieces = (
        lax.all_gather(joined_key_rows, "ctx", axis=0, tiled=True),
        lax.all_gather(joined_value_rows, "ctx", axis=0, tiled=True),
    )
    row_ids = jnp.arange(pieces[0].shape[0], dtype=jnp.int32)
    key_pos, key_live = key_layout(
        row_ids, prior_rows, prompt_slot_count, prior_total, devices, shard_counts, block_offsets
    )
    head_key_rows = pieces[0]
    head_value_rows = pieces[1]
    total_row_count = head_key_rows.shape[0]
    step_rows = total_row_count
    while step_rows > 1024 and step_rows % 2 == 0:
        step_rows = step_rows // 2
    blocks = total_row_count // step_rows
    block_inputs = (
        head_key_rows.reshape(blocks, step_rows, head_key_rows.shape[1]),
        head_value_rows.reshape(blocks, step_rows, head_value_rows.shape[1]),
        key_pos.reshape(blocks, step_rows),
        key_live.reshape(blocks, step_rows),
    )

    def scan_step(state_in, block_item):
        return (update(state_in, block_item[0], block_item[1], block_item[2], block_item[3]), None)

    final = lax.scan(scan_step, initial, block_inputs)[0]
    span_totals = final[1]
    span_mixture = final[2]
    span_out = jnp.where(
        query_live[:, None, None, None], span_mixture / span_totals[..., None], 0.0
    )
    span_out = span_out.reshape(prompt_slot_count, QUERY_HEADS * HEAD_WIDTH).astype(jnp.bfloat16)
    decoded_query_row = decoded_query.reshape(KEY_VALUE_HEADS, HEADS_PER_GROUP, HEAD_WIDTH)
    visible_key_count = joined_key_rows.shape[0]
    decode_scores = (
        jnp.einsum(
            "gqd,rgd->gqr",
            decoded_query_row,
            joined_key_rows.reshape(visible_key_count, KEY_VALUE_HEADS, HEAD_WIDTH),
            preferred_element_type=jnp.float32,
        )
        * logit_scale
    )
    local_live = jnp.concatenate([jnp.ones((prior_rows,), dtype=bool), query_live])
    decode_scores = jnp.where(local_live[None, None, :], decode_scores, NEGATIVE_FILL)
    local_peaks = jnp.max(decode_scores, axis=-1)
    local_weights = jnp.where(
        local_live[None, None, :], jnp.exp(decode_scores - local_peaks[..., None]), 0.0
    )
    local_totals = jnp.sum(local_weights, axis=-1)
    local_mix = jnp.einsum(
        "gqr,rgd->gqd",
        local_weights.astype(jnp.bfloat16),
        joined_value_rows.reshape(visible_key_count, KEY_VALUE_HEADS, HEAD_WIDTH),
        preferred_element_type=jnp.float32,
    )
    merged_peaks = lax.pmax(local_peaks, "ctx")
    factor = jnp.exp(local_peaks - merged_peaks)
    merged_totals, merged_mix = lax.psum(
        (factor * local_totals, factor[..., None] * local_mix), "ctx"
    )
    self_score = (
        jnp.einsum(
            "sop,sp->so",
            decoded_query_row,
            decoded_key.reshape(KEY_VALUE_HEADS, HEAD_WIDTH),
            preferred_element_type=jnp.float32,
        )
        * logit_scale
    )
    final_peaks = jnp.maximum(merged_peaks, self_score)
    keep_weight = jnp.exp(merged_peaks - final_peaks)
    self_weight = jnp.exp(self_score - final_peaks)
    numerator = keep_weight[..., None] * merged_mix + self_weight[
        ..., None
    ] * decoded_value.reshape(KEY_VALUE_HEADS, 1, HEAD_WIDTH).astype(jnp.float32)
    denominator = keep_weight * merged_totals + self_weight
    next_out = (
        (numerator / denominator[..., None]).reshape(QUERY_HEADS * HEAD_WIDTH).astype(jnp.bfloat16)
    )
    return (span_out, next_out)


def solution(mesh):
    in_specs = (
        P(("groups", "ctx"), None),
        P(("groups", "ctx"), None),
        P(("groups", "ctx"), None),
        P(("groups", "ctx"), None),
        P(("groups", "ctx"), None),
        P("groups"),
        P("groups"),
        P("groups"),
        P("groups", None),
        P("groups", None),
    )
    out_specs = (P(("groups", "ctx"), None), P("groups"))
    return jax.shard_map(body, mesh=mesh, in_specs=in_specs, out_specs=out_specs, check_vma=False)
```

profile of v0, /device:TPU:0, one launch (start us, length us, event | category | flops | bytes accessed | tf_op | source)
XLA Modules:
  0.0 139.5 jit_solution(3694339848404358911)
XLA Ops:
  7.2 0.7 constant_dynamic-update-slice_fusion.1
  7.9 0.8 constant_dynamic-update-slice_fusion
  8.8 0.6 copy-done.1
  9.4 0.0 all-gather.5.cloned.1.call-start
  9.5 0.7 constant_dynamic-update-slice_fusion.3
  10.2 0.8 constant_dynamic-update-slice_fusion.2
  11.0 0.6 copy-done.2
  11.7 0.8 slice_bitcast_fusion.1
  12.5 0.8 constant_dynamic-slice_fusion.2
  13.2 0.5 fusion.52
  13.8 0.1 select_reduce_fusion
  13.9 0.1 reduce_sum.69
  14.0 0.1 reduce_sum.67
  14.0 0.1 reduce_sum.65
  14.1 0.1 reduce_sum.63
  14.2 1.1 copy.35
  15.3 0.2 copy.21
  15.6 1.2 fusion.47
  16.8 0.1 concatenate.11
  16.9 1.1 fusion.54
  18.0 35.1 %pmax.7 = f32[4,8]{1,0:T(4,128)S(1)} all-reduce(f32[4,8]{1,0:T(4,128)S(1)} %get-tuple-element.166), channel_id=1, replica_groups=mesh['groups'=2,'ctx'=16] {'ctx'}, use_global_device_ids=true, to_apply=%region_9.10 | all-reduce | flops 32 | bytes 256 | tf_op jit(solution)/shard_map/pmax | solution.py:161
  53.1 0.2 fusion.29
  53.3 1.1 convolution_multiply_fusion
  54.3 57.8 %all-reduce.1 = (f32[4,8]{1,0:T(4,128)S(1)}, f32[4,8,128]{2,1,0:T(8,128)S(1)}) all-reduce(f32[4,8]{1,0:T(4,128)S(1)} %get-tuple-element.152, f32[4,8,128]{2,1,0:T(8,128)S(1)} %convolution_multiply_fusion), channel_id=1, replica_groups=mesh['groups'=2,'ctx'=16] {'ctx'}, use_global_device_ids=true, to_apply=%region_12.13 | all-reduce | flops 4128 | bytes 33024 | tf_op jit(solution)/shard_map/psum | solution.py:163
  112.2 0.6 fusion.53
  112.8 0.7 bitcast_convert_fusion
  113.4 0.8 fusion.34
  114.3 0.7 fusion.39
  115.0 15.9 %while.15 = (s32[]{:T(128)}, f32[64,4,8]{0,2,1:T(8,128)S(1)}, f32[64,4,8]{0,2,1:T(8,128)S(1)}, f32[64,4,8,128]{3,0,2,1:T(8,128)S(1)}, pred[2,576]{1,0:T(4,128)(4...) while((s32[]{:T(128)}, f32[64,4,8]{0,2,1:T(8,128)S(1)}, ...), condition=%wide.region_7.8_spmd.clone, body=%wide.region_4.7_spmd.clone.sunk | while | flops 620185984 | bytes 22963300 | solution.py:130
  115.0 1.2 fusion.69
  116.3 0.1 compare_and_fusion.2
  116.4 1.3 constant_dynamic-slice_fusion.5
  117.7 0.1 reshape.157
  117.9 0.1 reshape.158
  118.0 1.1 fusion.70
  119.2 1.8 %fusion.71 = f32[64,4,8]{0,2,1:T(8,128)S(1)} fusion(f32[4,576,64,8]{1,2,3,0:T(8,128)S(1)} %get-tuple-element.247, f32[64,4,8]{0,2,1:T(8,128)S(1)} %select_maximum_fusion.2, pred[64,576]{1,0:T(8,128)(4,1)S(1)} %compare_and_fusion.2), kind=kLoop, calls=%fused_computation.5.clone.1 | loop fusion | flops 5896192 | bytes 4771840 | tf_op jit(solution)/shard_map/while/body/eval_jaxpr/reduce_sum | solution.py:94
  121.0 2.0 %fusion.73 = f32[64,4,8,128]{3,0,2,1:T(8,128)S(1)} fusion(f32[4,576,64,8]{1,2,3,0:T(8,128)S(1)} %get-tuple-element.247, f32[64,4,8]{0,2,1:T(8,128)S(1)} %select_maximum_fusion.2, pred[64,576]{1,0:T(8,128)(4,1)S(1)} %compare_and_fusion.2, f32[64,4,8,128]{3,0,2,1:T(8,128)S(1)} %get-tuple-element.267, bf16[576,4,128,1]{2,1,0,3:T(4,128)(2,1)S(1)} %bitcast.94, ...), kind=kOutput, calls=%fused_computation.9.clone.1 | convolution fusion | flops 308674560 | bytes 7458817 | tf_op jit(solution)/shard_map/while/body/eval_jaxpr/tgqr,rgd->tgqd/dot_general | solution.py:86
  123.0 1.2 fusion.69
  124.2 0.1 compare_and_fusion.2
  124.3 1.3 constant_dynamic-slice_fusion.5
  125.7 0.1 reshape.157
  125.8 0.1 reshape.158
  126.0 1.1 fusion.70
  127.1 1.8 %fusion.71 = f32[64,4,8]{0,2,1:T(8,128)S(1)} fusion(f32[4,576,64,8]{1,2,3,0:T(8,128)S(1)} %get-tuple-element.247, f32[64,4,8]{0,2,1:T(8,128)S(1)} %select_maximum_fusion.2, pred[64,576]{1,0:T(8,128)(4,1)S(1)} %compare_and_fusion.2), kind=kLoop, calls=%fused_computation.5.clone.1 | loop fusion | flops 5896192 | bytes 4771840 | tf_op jit(solution)/shard_map/while/body/eval_jaxpr/reduce_sum | solution.py:94
  128.9 2.0 %fusion.73 = f32[64,4,8,128]{3,0,2,1:T(8,128)S(1)} fusion(f32[4,576,64,8]{1,2,3,0:T(8,128)S(1)} %get-tuple-element.247, f32[64,4,8]{0,2,1:T(8,128)S(1)} %select_maximum_fusion.2, pred[64,576]{1,0:T(8,128)(4,1)S(1)} %compare_and_fusion.2, f32[64,4,8,128]{3,0,2,1:T(8,128)S(1)} %get-tuple-element.267, bf16[576,4,128,1]{2,1,0,3:T(4,128)(2,1)S(1)} %bitcast.94, ...), kind=kOutput, calls=%fused_computation.9.clone.1 | convolution fusion | flops 308674560 | bytes 7458817 | tf_op jit(solution)/shard_map/while/body/eval_jaxpr/tgqr,rgd->tgqd/dot_general | solution.py:86
  130.9 0.4 select_convert_fusion
  131.3 0.3 copy.22
  131.6 1.0 copy.56
  (27 shorter events, 0.3 us)
Async XLA Ops:
  7.2 9.7 %copy-start = (bf16[4096]{0:T(1024)(128)(2,1)S(1)}, bf16[4096]{0:T(1024)(128)(2,1)}, u32[]{:S(2)}) copy-start(bf16[4096]{0:T(1024)(128)(2,1)} %param.17) | copy-start | bytes 24580
  7.2 107.8 %all-gather.3.cloned.1.call-start = ((), (), s32[]{:S(2)}) async-start(), calls=%async_computation | async-start | bytes 1253376 | tf_op jit(solution)/shard_map/all_gather | solution.py:106
  8.8 0.6 copy-start.1
  9.4 105.6 %all-gather.5.cloned.1.call-start = ((), (), s32[]{:S(2)}) async-start(), calls=%async_computation.1 | async-start | bytes 1253376 | tf_op jit(solution)/shard_map/all_gather | solution.py:107
  11.0 0.6 copy-start.2
Sparse Core Ops, SparseCore 0:
  10.8 41.0 all-gather.2
  54.2 37.2 all-gather.4
where the time goes:
time: 140 us; the launch traced here: 139 us
  blocking collectives  92.9 us (66%)
  between operations  14.2 us (10%)
  local copies, waits for them, and re-layouts  13.4 us (10%)
  other arithmetic  9.46 us (7%)
  matrix products  9.28 us (7%)
    psum x1, blocking collectives, body(): lax.psum((factor * local_totals, factor[..., None] * local_mix), 'ctx')  57.8 us
    pmax x1, blocking collectives, body(): merged_peaks = lax.pmax(local_peaks, 'ctx')  35.1 us
    unnamed x11, local copies, waits for them, and re-layouts  5.01 us
    dot_general x2, matrix products, update(): jnp.einsum('tgqr,rgd->tgqd', weights.astype(jnp.bfloat16), head_value_row...  3.98 us
    reduce_sum x2, other arithmetic, update(): jnp.sum(weights, axis=-1)  3.52 us
  transfers between devices with their start and end apart: 2, of which 0 were waited for; matrix products, arithmetic and copies ran while one was open for 9% of the time, Pallas kernels for 0%

commit v1 on v0

v1 whole, which is shorter than its diff:
```python
import functools

import jax
import jax.numpy as jnp
from jax import lax
from jax.experimental import pallas as pl
from jax.experimental.pallas import tpu as pltpu
from jax.sharding import PartitionSpec as P

HEAD_WIDTH = 128
PIECES = 2
CHUNK = 4
LOG2E = 1.4426950408889634
FILL = -1e30
FAR = 1 << 29


class Body:
    def __init__(self, n, q, dq, dk, dv, counts, offsets, kv, out, nxt, peak, acc):
        self.n, self.q, self.dq, self.dk, self.dv = n, q, dq, dk, dv
        self.counts, self.offsets, self.kv, self.out, self.nxt = counts, offsets, kv, out, nxt
        self.peak, self.acc = peak, acc
        self.rows = q.shape[0]
        self.half = self.rows // 2
        self.prior = (kv.shape[2] - 2 * self.rows) // 2
        self.groups = dk.shape[0]
        self.per_piece = self.groups // PIECES
        self.per_group = q.shape[1] // HEAD_WIDTH // self.groups
        self.tall = self.per_group * self.rows
        self.total = self.tall + self.per_piece * self.per_group
        self.rate = HEAD_WIDTH**-0.5 * LOG2E

    def init(self):
        self.peak[...] = jnp.full(self.peak.shape, FILL, jnp.float32)
        self.acc[...] = jnp.zeros(self.acc.shape, jnp.float32)

    def query_positions(self, me):
        r = lax.broadcasted_iota(jnp.int32, (self.rows, 1), 0)
        second = r >= self.half
        offset = jnp.where(second, r - self.half, r)
        position = offset + jnp.where(second, self.offsets[1, me], self.offsets[0, me])
        live = offset < jnp.where(second, self.counts[1, me], self.counts[0, me])
        return position, live

    def bias(self, me, first):
        width = CHUNK * self.rows
        lane = lax.broadcasted_iota(jnp.int32, (1, width), 1)
        piece = lane // self.half
        offset = lane % self.half
        start = jnp.zeros((1, width), jnp.int32)
        count = jnp.zeros((1, width), jnp.int32)
        for i in range(CHUNK):
            for h in range(2):
                here = piece == 2 * i + h
                start = jnp.where(here, self.offsets[h, first + i], start)
                count = jnp.where(here, self.counts[h, first + i], count)
        position = jnp.where(offset < count, start + offset, FAR)
        own, _ = self.query_positions(me)
        span = jnp.where(position <= own, 0.0, FILL).astype(jnp.float32)
        step = jnp.where(position < FAR, 0.0, FILL).astype(jnp.float32)
        return span, step

    def queries(self, g):
        base = g * self.per_group
        parts = [
            self.q[:, (base + h) * HEAD_WIDTH : (base + h + 1) * HEAD_WIDTH]
            for h in range(self.per_group)
        ]
        piece_rows = self.per_piece * self.per_group
        top = (g // self.per_piece) * piece_rows
        parts.append(self.dq[top : top + piece_rows, :])
        return jnp.concatenate(parts, axis=0)

    def chunk_rows(self, g, first, start):
        j = g % self.per_piece
        block = self.kv[
            g // self.per_piece,
            pl.ds(first, CHUNK),
            start : start + self.rows,
            j * HEAD_WIDTH : (j + 1) * HEAD_WIDTH,
        ]
        return block.reshape(CHUNK * self.rows, HEAD_WIDTH)

    def prefix_rows(self, g, first, devices):
        j = g % self.per_piece
        block = self.kv[
            g // self.per_piece,
            pl.ds(first, devices),
            2 * self.rows :,
            j * HEAD_WIDTH : (j + 1) * HEAD_WIDTH,
        ].astype(jnp.float32)
        flat = (devices * self.prior, HEAD_WIDTH)
        keys = block[:, : self.prior].reshape(flat).astype(jnp.bfloat16)
        values = block[:, self.prior :].reshape(flat).astype(jnp.bfloat16)
        return keys, values

    def update(self, g, keys, values, masks):
        scores = lax.dot_general(
            self.queries(g), keys, (((1,), (1,)), ((), ())), preferred_element_type=jnp.float32
        )
        if masks is not None:
            span, step = masks
            width = span.shape[1]
            extra = scores.shape[1] - width
            if extra:
                span = jnp.concatenate([span, jnp.zeros((span.shape[0], extra), jnp.float32)], 1)
                step = jnp.concatenate([step, jnp.zeros((1, extra), jnp.float32)], 1)
            low = jnp.broadcast_to(step, (self.total - self.tall, step.shape[1]))
            scores = scores + jnp.concatenate([span] * self.per_group + [low], 0)
        old = self.peak[g]
        new = jnp.maximum(old, jnp.max(scores, axis=1, keepdims=True))
        weights = jnp.exp2((scores - new[:, :1]) * self.rate).astype(jnp.bfloat16)
        wide = jnp.concatenate([values, jnp.ones(values.shape, jnp.bfloat16)], 1)
        summed = jnp.dot(weights, wide, preferred_element_type=jnp.float32)
        scale = jnp.exp2((old - new) * self.rate)
        self.acc[g] = self.acc[g] * jnp.concatenate([scale, scale], 1) + summed
        self.peak[g] = new

    def chunk(self, g, first, masks, prefix):
        keys = self.chunk_rows(g, first, 0)
        values = self.chunk_rows(g, first, self.rows)
        if prefix:
            more_keys, more_values = self.prefix_rows(g, 0, self.n)
            keys = jnp.concatenate([keys, more_keys], 0)
            values = jnp.concatenate([values, more_values], 0)
        self.update(g, keys, values, masks)

    def finish(self, g, me):
        _, live = self.query_positions(me)
        base = g * self.per_group
        for h in range(self.per_group):
            part = self.acc[g, h * self.rows : (h + 1) * self.rows, :]
            result = part[:, :HEAD_WIDTH] / part[:, HEAD_WIDTH:]
            result = jnp.where(live, result, 0.0).astype(jnp.bfloat16)
            self.out[:, (base + h) * HEAD_WIDTH : (base + h + 1) * HEAD_WIDTH] = result

    def finish_step(self, piece):
        results = []
        for j in range(self.per_piece):
            g = piece * self.per_piece + j
            top = self.tall + j * self.per_group
            part = self.acc[g, top : top + self.per_group, :]
            old = self.peak[g, top : top + self.per_group, :]
            rows = self.per_piece * self.per_group
            query = self.dq[piece * rows : (piece + 1) * rows, :].astype(jnp.float32)
            query = query[j * self.per_group : (j + 1) * self.per_group]
            key = self.dk[g : g + 1, :].astype(jnp.float32)
            value = self.dv[g : g + 1, :].astype(jnp.float32)
            score = jnp.sum(query * key, axis=1, keepdims=True)
            new = jnp.maximum(old, score)
            keep = jnp.exp2((old - new) * self.rate)
            own = jnp.exp2((score - new) * self.rate)
            top_sum = keep * part[:, :HEAD_WIDTH] + own * value
            results.append(top_sum / (keep * part[:, HEAD_WIDTH:] + own))
        rows = self.per_piece * self.per_group
        self.nxt[piece * rows : (piece + 1) * rows, :] = jnp.concatenate(results, 0).astype(
            jnp.bfloat16
        )


def ring_kernel(
    n,
    counts,
    offsets,
    pk,
    pv,
    ck,
    cv,
    q_hbm,
    dq,
    dk,
    dv,
    out,
    nxt,
    kv,
    q,
    peak,
    acc,
    sends,
    recvs,
    local,
):
    me = lax.axis_index("ctx")
    lines = n // CHUNK
    z, x, c = me // CHUNK, (me // 2) % 2, me % 2
    last = lines - 1
    half = kv.shape[3]
    own_copies = []
    for p in range(PIECES):
        top = 0
        for i, source in enumerate((pk, pv, ck, cv)):
            rows = source.shape[0]
            own_copies.append(
                pltpu.make_async_copy(
                    source.at[:, p * half : (p + 1) * half],
                    kv.at[p, me, top : top + rows],
                    local.at[4 * p + i],
                )
            )
            top += rows
    for d in own_copies:
        d.start()
    q_copy = pltpu.make_async_copy(q_hbm, q, local.at[8])
    q_copy.start()
    to_x = z * CHUNK + (1 - x) * 2 + c
    to_core = z * CHUNK + x * 2 + (1 - c)
    targets = (me + CHUNK, me - CHUNK, to_x, to_core)

    barrier = pltpu.get_barrier_semaphore()

    def greet(target):
        pl.semaphore_signal(
            barrier, inc=1, device_id={"ctx": target}, device_id_type=pl.DeviceIdType.MESH
        )

    greet(to_x)
    greet(to_core)

    @pl.when(z < last)
    def _():
        greet(me + CHUNK)

    @pl.when(z > 0)
    def _():
        greet(me - CHUNK)

    inner = jnp.where((z > 0) & (z < last), 1, 0).astype(jnp.int32)
    pl.semaphore_wait(barrier, 3 + inner)

    def copy(way, source, p):
        return pltpu.make_async_remote_copy(
            src_ref=kv.at[p, source],
            dst_ref=kv.at[p, source],
            send_sem=sends.at[way, source, p],
            recv_sem=recvs.at[source, p],
            device_id={"ctx": targets[way]},
            device_id_type=pl.DeviceIdType.MESH,
        )

    def column(line):
        return line * CHUNK + x * 2 + c

    def spread(line, p, act):
        @pl.when((line <= z) & (z < last))
        def _():
            act(copy(0, column(line), p))

        @pl.when((line >= z) & (z > 0))
        def _():
            act(copy(1, column(line), p))

        act(copy(2, column(line), p))
        act(copy(3, column(line), p))

    def other(line):
        return line * CHUNK + (1 - x) * 2 + c

    def start(d):
        d.start()

    near = jnp.minimum(z, last - z)
    lower = z < lines // 2
    order = []
    for s in range(lines):
        base = s if s >= 2 else (near if s == 0 else 1 - near)
        order.append(jnp.where(lower, base, last - base))

    for p in range(PIECES):
        for d in own_copies[4 * p : 4 * p + 4]:
            d.wait()
        spread(z, p, start)

    body = Body(n, q, dq, dk, dv, counts, offsets, kv, out, nxt, peak, acc)
    body.init()

    def from_column(s, p):
        copy(2, column(order[s]), p).wait_recv()
        spread(order[s], p, start)

    def from_x(s, p):
        copy(3, other(order[s]), p).wait_recv()
        copy(3, other(order[s]), p).start()

    def from_core(s, p):
        for side in range(2):
            copy(2, order[s] * CHUNK + side * 2 + (1 - c), p).wait_recv()

    for p in range(PIECES):
        from_column(1, p)
        from_x(0, p)
    q_copy.wait()
    for s in range(lines):
        final = s == lines - 1
        masks = body.bias(me, order[s] * CHUNK)
        for p in range(PIECES):
            if s + 2 < lines:
                from_column(s + 2, p)
            from_core(s, p)
            for j in range(body.per_piece):
                body.chunk(p * body.per_piece + j, order[s] * CHUNK, masks, final)
            if s + 1 < lines:
                from_x(s + 1, p)
            if final:
                for j in range(body.per_piece):
                    body.finish(p * body.per_piece + j, me)
                body.finish_step(p)
    for s in range(lines):
        for p in range(PIECES):
            spread(order[s], p, lambda d: d.wait_send())
            copy(3, other(order[s]), p).wait_send()


def local_kernel(n, counts, offsets, kv, q, dq, dk, dv, out, nxt, peak, acc):
    me = lax.axis_index("ctx")
    body = Body(n, q, dq, dk, dv, counts, offsets, kv, out, nxt, peak, acc)
    body.init()
    devices = HEAD_WIDTH // body.prior
    for g in range(body.groups):

        def step(i, carry):
            body.chunk(g, i * CHUNK, body.bias(me, i * CHUNK), False)
            return carry

        def prefix_step(i, carry):
            keys, values = body.prefix_rows(g, i * devices, devices)
            body.update(g, keys, values, None)
            return carry

        lax.fori_loop(0, n // CHUNK, step, 0)
        lax.fori_loop(0, n // devices, prefix_step, 0)
        body.finish(g, me)
    for p in range(PIECES):
        body.finish_step(p)


def body_fn(
    prompt_query,
    prompt_key,
    prompt_value,
    prefix_key_cache,
    prefix_value_cache,
    decoded_query,
    decoded_key,
    decoded_value,
    shard_counts,
    block_offsets,
):
    n = lax.axis_size("ctx")
    rows = prompt_query.shape[0]
    groups = prompt_key.shape[1] // HEAD_WIDTH
    heads = prompt_query.shape[1] // HEAD_WIDTH
    blocks = (prompt_key, prompt_value, prefix_key_cache, prefix_value_cache)
    tables = (shard_counts.T, block_offsets.T)
    half = prompt_key.shape[1] // PIECES
    height = sum(b.shape[0] for b in blocks)
    dq = decoded_query.reshape(heads, HEAD_WIDTH)
    dk = decoded_key.reshape(groups, HEAD_WIDTH)
    dv = decoded_value.reshape(groups, HEAD_WIDTH)
    total = heads // groups * rows + heads // PIECES
    smem = pl.BlockSpec(memory_space=pltpu.SMEM)
    vmem = pl.BlockSpec(memory_space=pltpu.VMEM)
    hbm = pl.BlockSpec(memory_space=pl.ANY)
    out_shape = (
        jax.ShapeDtypeStruct(prompt_query.shape, jnp.bfloat16),
        jax.ShapeDtypeStruct((heads, HEAD_WIDTH), jnp.bfloat16),
    )
    state = [
        pltpu.VMEM((groups, total, HEAD_WIDTH), jnp.float32),
        pltpu.VMEM((groups, total, 2 * HEAD_WIDTH), jnp.float32),
    ]
    if n == 4 * CHUNK:
        span, nxt = pl.pallas_call(
            functools.partial(ring_kernel, n),
            out_shape=out_shape,
            in_specs=[smem, smem, hbm, hbm, hbm, hbm, hbm, vmem, vmem, vmem],
            out_specs=(vmem, vmem),
            scratch_shapes=[
                pltpu.VMEM((PIECES, n, height, half), jnp.bfloat16),
                pltpu.VMEM(prompt_query.shape, jnp.bfloat16),
                *state,
                pltpu.SemaphoreType.DMA((4, n, PIECES)),
                pltpu.SemaphoreType.DMA((n, PIECES)),
                pltpu.SemaphoreType.DMA((9,)),
            ],
            compiler_params=pltpu.CompilerParams(
                collective_id=0, has_side_effects=True, vmem_limit_bytes=48 * 1024 * 1024
            ),
        )(*tables, *blocks, prompt_query, dq, dk, dv)
    else:
        joined = jnp.concatenate(blocks, axis=0)
        joined = jnp.stack([joined[:, p * half : (p + 1) * half] for p in range(PIECES)], 0)
        gathered = lax.all_gather(joined, "ctx", axis=1)
        span, nxt = pl.pallas_call(
            functools.partial(local_kernel, n),
            out_shape=out_shape,
            in_specs=[smem, smem, vmem, vmem, vmem, vmem, vmem],
            out_specs=(vmem, vmem),
            scratch_shapes=state,
            compiler_params=pltpu.CompilerParams(vmem_limit_bytes=56 * 1024 * 1024),
        )(*tables, gathered, prompt_query, dq, dk, dv)
    return span, nxt.reshape(heads * HEAD_WIDTH)


def solution(mesh):
    both = P(("groups", "ctx"), None)
    in_specs = (
        both,
        both,
        both,
        both,
        both,
        P("groups"),
        P("groups"),
        P("groups"),
        P("groups", None),
        P("groups", None),
    )
    out_specs = (both, P("groups"))
    return jax.shard_map(
        body_fn, mesh=mesh, in_specs=in_specs, out_specs=out_specs, check_vma=False
    )
```

time: 140 us -> 36 us (0.26)
  blocking collectives: 92.9 us -> 0 us
  Pallas kernels: 0 us -> 26.7 us
  between operations: 14.2 us -> 0.67 us
  other arithmetic: 9.46 us -> 0 us
  matrix products: 9.28 us -> 0 us
  local copies, waits for them, and re-layouts: 13.4 us -> 8.23 us
    psum x1 -> x0, blocking collectives: 57.8 us -> none  [body(): lax.psum((factor * local_totals, factor[..., None] * local_mix), 'ctx')]
    pmax x1 -> x0, blocking collectives: 35.1 us -> none  [body(): merged_peaks = lax.pmax(local_peaks, 'ctx')]
    pallas_call x0 -> x1, Pallas kernels: none -> 26.7 us  [body_fn(): pl.pallas_call(functools.partial(ring_kernel, n), out_shape=out_shape, in...]
    dot_general x7 -> x0, matrix products: 9.28 us -> none  [the longest x2 3.98 us: update(): jnp.einsum('tgqr,rgd->tgqd', weights.astype(jnp.bfloat16), head_value_row...]
    reduce_sum x4 -> x0, other arithmetic: 3.8 us -> none  [the longest x2 3.52 us: update(): jnp.sum(weights, axis=-1)]
    dynamic_slice x7 -> x0, local copies, waits for them, and re-layouts: 3.52 us -> none  [the longest x6 2.75 us: body(): final = lax.scan(scan_step, initial, block_inputs)[0]]
    unnamed x11 -> x22, local copies, waits for them, and re-layouts: 5.01 us -> 8.23 us
    add x5 -> x0, other arithmetic: 2.42 us -> none  [the longest x2 2.38 us: body(): prior_total + jnp.where(second, own_offsets[1], own_offsets[0]) + offset_in]
  transfers between devices with their start and end apart: 2 -> 0, of which waited for: 0 -> 0; matrix products, arithmetic and copies ran while one was open for 9% -> 0% of each run, Pallas kernels for 0% -> 0%
where the time goes in v1:
time: 36 us; the launch traced here: 35.5 us
  Pallas kernels  26.7 us (74%)
  local copies, waits for them, and re-layouts  8.23 us (23%)
  between operations  0.67 us (2%)
    pallas_call x1, Pallas kernels, body_fn(): pl.pallas_call(functools.partial(ring_kernel, n), out_shape=out_shape, in...  26.7 us
    unnamed x22, local copies, waits for them, and re-layouts  8.23 us

profile of v1, /device:TPU:0, one launch (start us, length us, event | category | flops | bytes accessed | tf_op | source)
XLA Modules:
  0.0 35.5 jit_solution(13043508823613770420)
XLA Ops:
  0.6 0.0 copy-start.3
  0.6 0.0 copy-start.6
  0.7 0.7 %copy-done.3 = bf16[8,512]{1,0:T(8,128)(2,1)S(1)} copy-done((bf16[8,512]{1,0:T(8,128)(2,1)S(1)}, bf16[8,512]{1,0:T(8,128)(2,1)}, u32[]{:S(2)}) %copy-start.3) | copy-done | bytes 8216
  1.3 0.0 copy-done.6
  1.3 0.0 copy-start
  1.3 1.0 %copy-done = bf16[64,4096]{1,0:T(8,128)(2,1)S(1)} copy-done((bf16[64,4096]{1,0:T(8,128)(2,1)S(1)}, bf16[64,4096]{1,0:T(8,128)(2,1)}, u32[]{:S(2)}) %copy-start) | copy-done | bytes 524312
  2.4 0.0 copy-start.1
  2.4 0.8 %copy-done.1 = bf16[64,512]{1,0:T(8,128)(2,1)S(1)} copy-done((bf16[64,512]{1,0:T(8,128)(2,1)S(1)}, bf16[64,512]{1,0:T(8,128)(2,1)}, u32[]{:S(2)}) %copy-start.1) | copy-done | bytes 65560
  3.2 0.0 copy-start.2
  3.2 0.8 %copy-done.2 = bf16[64,512]{1,0:T(8,128)(2,1)S(1)} copy-done((bf16[64,512]{1,0:T(8,128)(2,1)S(1)}, bf16[64,512]{1,0:T(8,128)(2,1)}, u32[]{:S(2)}) %copy-start.2) | copy-done | bytes 65560
  4.1 0.0 copy-start.4
  4.1 0.7 %copy-done.4 = bf16[8,512]{1,0:T(8,128)(2,1)S(1)} copy-done((bf16[8,512]{1,0:T(8,128)(2,1)S(1)}, bf16[8,512]{1,0:T(8,128)(2,1)}, u32[]{:S(2)}) %copy-start.4) | copy-done | bytes 8216
  4.8 0.0 copy-start.5
  4.8 0.7 %copy-done.5 = bf16[4096]{0:T(1024)(128)(2,1)S(1)} copy-done((bf16[4096]{0:T(1024)(128)(2,1)S(1)}, bf16[4096]{0:T(1024)(128)(2,1)}, u32[]{:S(2)}) %copy-start.5) | copy-done | bytes 8216
  5.5 0.0 copy-start.7
  5.5 0.7 %copy-done.7 = s32[16,2]{0,1:T(2,128)S(1)} copy-done((s32[16,2]{0,1:T(2,128)S(1)}, s32[16,2]{0,1:T(2,128)}, u32[]{:S(2)}) %copy-start.7) | copy-done | bytes 152
  6.1 0.0 copy-start.8
  6.1 0.7 %copy-done.8 = bf16[512]{0:T(512)(128)(2,1)S(1)} copy-done((bf16[512]{0:T(512)(128)(2,1)S(1)}, bf16[512]{0:T(512)(128)(2,1)}, u32[]{:S(2)}) %copy-start.8) | copy-done | bytes 1048
  6.8 0.0 copy-start.9
  6.8 0.7 %copy-done.9 = bf16[512]{0:T(512)(128)(2,1)S(1)} copy-done((bf16[512]{0:T(512)(128)(2,1)S(1)}, bf16[512]{0:T(512)(128)(2,1)}, u32[]{:S(2)}) %copy-start.9) | copy-done | bytes 1048
  7.5 26.7 %shard_map.113 = (bf16[64,4096]{1,0:T(8,128)(2,1)S(1)}, bf16[32,128]{1,0:T(8,128)(2,1)S(1)}) custom-call(s32[2,16]{1,0:T(2,128)S(1)} %bitcast.8, s32[2,16]{1,0:T(2,128)S(1)} %bitcast.9, bf16[64,512]{1,0:T(8,128)(2,1)S(1)} %copy-done.1, bf16[64,512]{1,0:T(8,128)(2,1)S(1)} %copy-done.2, bf16[8,512]{1,0:T(8,128)(2,1)S(1)} %copy-done.3, ...), custom_call_target="tpu_custom_call" | custom-call | tf_op jit(solution)/shard_map/pallas_call | solution.py:372
  34.2 0.8 %copy.14 = bf16[64,4096]{1,0:T(8,128)(2,1)} copy(bf16[64,4096]{1,0:T(8,128)(2,1)S(1)} %get-tuple-element.8) | data formatting | bytes 1048576
  34.9 0.6 %copy.15 = bf16[4096]{0:T(1024)(128)(2,1)} copy(bf16[4096]{0:T(1024)(128)(2,1)S(1)} %bitcast.7) | data formatting | bytes 16384
Async XLA Ops:
  0.6 0.7 %copy-start.3 = (bf16[8,512]{1,0:T(8,128)(2,1)S(1)}, bf16[8,512]{1,0:T(8,128)(2,1)}, u32[]{:S(2)}) copy-start(bf16[8,512]{1,0:T(8,128)(2,1)} %ck.1) | copy-start | bytes 24580
  0.6 0.7 %copy-start.6 = (s32[16,2]{0,1:T(2,128)S(1)}, s32[16,2]{0,1:T(2,128)}, u32[]{:S(2)}) copy-start(s32[16,2]{0,1:T(2,128)} %param.18) | copy-start | bytes 388
  1.3 1.0 %copy-start = (bf16[64,4096]{1,0:T(8,128)(2,1)S(1)}, bf16[64,4096]{1,0:T(8,128)(2,1)}, u32[]{:S(2)}) copy-start(bf16[64,4096]{1,0:T(8,128)(2,1)} %q_hbm.1) | copy-start | bytes 1572868
  2.4 0.8 %copy-start.1 = (bf16[64,512]{1,0:T(8,128)(2,1)S(1)}, bf16[64,512]{1,0:T(8,128)(2,1)}, u32[]{:S(2)}) copy-start(bf16[64,512]{1,0:T(8,128)(2,1)} %pk.1) | copy-start | bytes 196612
  3.2 0.8 %copy-start.2 = (bf16[64,512]{1,0:T(8,128)(2,1)S(1)}, bf16[64,512]{1,0:T(8,128)(2,1)}, u32[]{:S(2)}) copy-start(bf16[64,512]{1,0:T(8,128)(2,1)} %pv.1) | copy-start | bytes 196612
  4.1 0.7 %copy-start.4 = (bf16[8,512]{1,0:T(8,128)(2,1)S(1)}, bf16[8,512]{1,0:T(8,128)(2,1)}, u32[]{:S(2)}) copy-start(bf16[8,512]{1,0:T(8,128)(2,1)} %cv.1) | copy-start | bytes 24580
  4.8 0.7 %copy-start.5 = (bf16[4096]{0:T(1024)(128)(2,1)S(1)}, bf16[4096]{0:T(1024)(128)(2,1)}, u32[]{:S(2)}) copy-start(bf16[4096]{0:T(1024)(128)(2,1)} %param.15) | copy-start | bytes 24580
  5.5 0.7 %copy-start.7 = (s32[16,2]{0,1:T(2,128)S(1)}, s32[16,2]{0,1:T(2,128)}, u32[]{:S(2)}) copy-start(s32[16,2]{0,1:T(2,128)} %param.19) | copy-start | bytes 388
  6.1 0.7 %copy-start.8 = (bf16[512]{0:T(512)(128)(2,1)S(1)}, bf16[512]{0:T(512)(128)(2,1)}, u32[]{:S(2)}) copy-start(bf16[512]{0:T(512)(128)(2,1)} %param.16) | copy-start | bytes 3076
  6.8 0.7 %copy-start.9 = (bf16[512]{0:T(512)(128)(2,1)S(1)}, bf16[512]{0:T(512)(128)(2,1)}, u32[]{:S(2)}) copy-start(bf16[512]{0:T(512)(128)(2,1)} %param.17) | copy-start | bytes 3076

commit v2 on v1

--- a/solution.py
+++ b/solution.py
@@ -167,13 +167,16 @@
     ck,
     cv,
     q_hbm,
-    dq,
-    dk,
-    dv,
+    dq_hbm,
+    dk_hbm,
+    dv_hbm,
     out,
     nxt,
     kv,
     q,
+    dq,
+    dk,
+    dv,
     peak,
     acc,
     sends,
@@ -200,8 +203,14 @@
             top += rows
     for d in own_copies:
         d.start()
-    q_copy = pltpu.make_async_copy(q_hbm, q, local.at[8])
-    q_copy.start()
+    query_copies = [
+        pltpu.make_async_copy(source, target, local.at[8 + i])
+        for i, (source, target) in enumerate(
+            ((q_hbm, q), (dq_hbm, dq), (dk_hbm, dk), (dv_hbm, dv))
+        )
+    ]
+    for d in query_copies:
+        d.start()
     to_x = z * CHUNK + (1 - x) * 2 + c
     to_core = z * CHUNK + x * 2 + (1 - c)
     targets = (me + CHUNK, me - CHUNK, to_x, to_core)
@@ -288,7 +297,8 @@
     for p in range(PIECES):
         from_column(1, p)
         from_x(0, p)
-    q_copy.wait()
+    for d in query_copies:
+        d.wait()
     for s in range(lines):
         final = s == lines - 1
         masks = body.bias(me, order[s] * CHUNK)
@@ -359,7 +369,7 @@
     total = heads // groups * rows + heads // PIECES
     smem = pl.BlockSpec(memory_space=pltpu.SMEM)
     vmem = pl.BlockSpec(memory_space=pltpu.VMEM)
-    hbm = pl.BlockSpec(memory_space=pl.ANY)
+    hbm = pl.BlockSpec(memory_space=pltpu.HBM)
     out_shape = (
         jax.ShapeDtypeStruct(prompt_query.shape, jnp.bfloat16),
         jax.ShapeDtypeStruct((heads, HEAD_WIDTH), jnp.bfloat16),
@@ -372,18 +382,21 @@
         span, nxt = pl.pallas_call(
             functools.partial(ring_kernel, n),
             out_shape=out_shape,
-            in_specs=[smem, smem, hbm, hbm, hbm, hbm, hbm, vmem, vmem, vmem],
+            in_specs=[smem, smem] + [hbm] * 8,
             out_specs=(vmem, vmem),
             scratch_shapes=[
                 pltpu.VMEM((PIECES, n, height, half), jnp.bfloat16),
                 pltpu.VMEM(prompt_query.shape, jnp.bfloat16),
+                pltpu.VMEM(dq.shape, jnp.bfloat16),
+                pltpu.VMEM(dk.shape, jnp.bfloat16),
+                pltpu.VMEM(dv.shape, jnp.bfloat16),
                 *state,
                 pltpu.SemaphoreType.DMA((4, n, PIECES)),
                 pltpu.SemaphoreType.DMA((n, PIECES)),
-                pltpu.SemaphoreType.DMA((9,)),
+                pltpu.SemaphoreType.DMA((12,)),
             ],
             compiler_params=pltpu.CompilerParams(
-                collective_id=0, has_side_effects=True, vmem_limit_bytes=48 * 1024 * 1024
+                collective_id=0, has_side_effects=True, vmem_limit_bytes=63 * 1024 * 1024
             ),
         )(*tables, *blocks, prompt_query, dq, dk, dv)
     else:

time: 36 us -> 30.9 us (0.86)
  local copies, waits for them, and re-layouts: 8.23 us -> 2.48 us
  Pallas kernels: 26.7 us -> 27.6 us
    unnamed x22 -> x4, local copies, waits for them, and re-layouts: 8.23 us -> 2.48 us
    pallas_call x1, Pallas kernels: 26.7 us -> 27.6 us  [body_fn(): pl.pallas_call(functools.partial(ring_kernel, n), out_shape=out_shape, in...]
where the time goes in v2:
time: 30.9 us; the launch traced here: 30.7 us
  Pallas kernels  27.6 us (89%)
  local copies, waits for them, and re-layouts  2.48 us (8%)
  between operations  0.65 us (2%)
    pallas_call x1, Pallas kernels, body_fn(): pl.pallas_call(functools.partial(ring_kernel, n), out_shape=out_shape, in...  27.6 us
    unnamed x4, local copies, waits for them, and re-layouts  2.48 us

profile of v2, /device:TPU:0, one launch (start us, length us, event | category | flops | bytes accessed | tf_op | source)
XLA Modules:
  0.0 30.7 jit_solution(1817886045284441631)
XLA Ops:
  0.6 27.6 %shard_map.113 = (bf16[64,4096]{1,0:T(8,128)(2,1)}, bf16[32,128]{1,0:T(8,128)(2,1)}) custom-call(s32[2,16]{1,0:T(2,128)} %bitcast.8, s32[2,16]{1,0:T(2,128)} %bitcast.9, bf16[64,512]{1,0:T(8,128)(2,1)} %pk.1, bf16[64,512]{1,0:T(8,128)(2,1)} %pv.1, bf16[8,512]{1,0:T(8,128)(2,1)} %ck.1, bf16[8,512]{1,0:T(8,128)(2,1)} %cv.1, bf16[64,4096]{1,0:T(8,128)(2,1)} %q_hbm.1, ...), custom_call_target="tpu_custom_call" | custom-call | tf_op jit(solution)/shard_map/pallas_call | solution.py:382
  28.2 0.0 copy-start
  28.2 1.9 %copy.14 = bf16[64,4096]{1,0:T(8,128)(2,1)} copy(bf16[64,4096]{1,0:T(8,128)(2,1)} %get-tuple-element.8) | data formatting | bytes 1048576
  30.1 0.0 copy-done
  30.1 0.6 %copy.15 = bf16[4096]{0:T(1024)(128)(2,1)} copy(bf16[4096]{0:T(1024)(128)(2,1)S(1)} %bitcast.7) | data formatting | bytes 16384
Async XLA Ops:
  28.2 1.9 %copy-start = (bf16[32,128]{1,0:T(8,128)(2,1)S(1)}, bf16[32,128]{1,0:T(8,128)(2,1)}, u32[]{:S(2)}) copy-start(bf16[32,128]{1,0:T(8,128)(2,1)} %get-tuple-element.5) | copy-start | bytes 24580

commit v3 on v2

--- a/solution.py
+++ b/solution.py
@@ -13,6 +13,26 @@
 LOG2E = 1.4426950408889634
 FILL = -1e30
 FAR = 1 << 29
+PLAN = (
+    ("further", 0, (0,)),
+    ("attend", 0, (0,)),
+    ("x", 1, (0,)),
+    ("further", 0, (1,)),
+    ("attend", 0, (1,)),
+    ("x", 1, (1,)),
+    ("last", 0, (0,)),
+    ("attend", 1, (0,)),
+    ("x", 2, (0,)),
+    ("last", 0, (1,)),
+    ("attend", 1, (1,)),
+    ("x", 2, (1,)),
+    ("attend", 2, (0,)),
+    ("x", 3, (0,)),
+    ("attend", 2, (1,)),
+    ("x", 3, (1,)),
+    ("attend", 3, (0,)),
+    ("attend", 3, (1,)),
+)
 
 
 class Body:
@@ -179,6 +199,8 @@
     dv,
     peak,
     acc,
+    spans,
+    steps,
     sends,
     recvs,
     local,
@@ -204,7 +226,7 @@
     for d in own_copies:
         d.start()
     query_copies = [
-        pltpu.make_async_copy(source, target, local.at[8 + i])
+        pltpu.make_async_copy(source, target, local.at[4 * PIECES + i])
         for i, (source, target) in enumerate(
             ((q_hbm, q), (dq_hbm, dq), (dk_hbm, dk), (dv_hbm, dv))
         )
@@ -249,7 +271,7 @@
     def column(line):
         return line * CHUNK + x * 2 + c
 
-    def spread(line, p, act):
+    def along(line, p, act):
         @pl.when((line <= z) & (z < last))
         def _():
             act(copy(0, column(line), p))
@@ -258,8 +280,13 @@
         def _():
             act(copy(1, column(line), p))
 
+    def across(line, p, act):
         act(copy(2, column(line), p))
         act(copy(3, column(line), p))
+
+    def spread(line, p, act):
+        along(line, p, act)
+        across(line, p, act)
 
     def other(line):
         return line * CHUNK + (1 - x) * 2 + c
@@ -280,11 +307,13 @@
         spread(z, p, start)
 
     body = Body(n, q, dq, dk, dv, counts, offsets, kv, out, nxt, peak, acc)
-    body.init()
-
-    def from_column(s, p):
-        copy(2, column(order[s]), p).wait_recv()
-        spread(order[s], p, start)
+
+    def arrived(line, p):
+        copy(2, column(line), p).wait_recv()
+
+    def from_column(line, p):
+        arrived(line, p)
+        spread(line, p, start)
 
     def from_x(s, p):
         copy(3, other(order[s]), p).wait_recv()
@@ -294,26 +323,58 @@
         for side in range(2):
             copy(2, order[s] * CHUNK + side * 2 + (1 - c), p).wait_recv()
 
-    for p in range(PIECES):
-        from_column(1, p)
-        from_x(0, p)
-    for d in query_copies:
-        d.wait()
-    for s in range(lines):
-        final = s == lines - 1
-        masks = body.bias(me, order[s] * CHUNK)
-        for p in range(PIECES):
-            if s + 2 < lines:
-                from_column(s + 2, p)
+    def attend(s, pieces):
+        for p in pieces:
             from_core(s, p)
+        masks = (spans[s], steps[s])
+        for p in pieces:
             for j in range(body.per_piece):
-                body.chunk(p * body.per_piece + j, order[s] * CHUNK, masks, final)
-            if s + 1 < lines:
-                from_x(s + 1, p)
-            if final:
+                body.chunk(p * body.per_piece + j, order[s] * CHUNK, masks, s == lines - 1)
+        if s == lines - 1:
+            for p in pieces:
                 for j in range(body.per_piece):
                     body.finish(p * body.per_piece + j, me)
                 body.finish_step(p)
+
+    def only(condition, act, *args):
+        @pl.when(condition)
+        def _():
+            act(*args)
+
+    inside = near == 1
+    outside = near == 0
+    for p in range(PIECES):
+        from_column(order[1], p)
+
+        @pl.when(inside)
+        def _():
+            arrived(order[2], p)
+            along(order[2], p, start)
+
+        from_x(0, p)
+        if p == 0:
+            for d in query_copies:
+                d.wait()
+            body.init()
+            for s in range(lines):
+                spans[s], steps[s] = body.bias(me, order[s] * CHUNK)
+
+    @pl.when(inside)
+    def _():
+        for p in range(PIECES):
+            across(order[2], p, start)
+
+    further = jnp.where(inside, order[3], order[2])
+    for kind, s, pieces in PLAN:
+        if kind == "attend":
+            attend(s, pieces)
+        for p in pieces:
+            if kind == "further":
+                from_column(further, p)
+            if kind == "last":
+                only(outside, from_column, order[lines - 1], p)
+            if kind == "x":
+                from_x(s, p)
     for s in range(lines):
         for p in range(PIECES):
             spread(order[s], p, lambda d: d.wait_send())
@@ -391,9 +452,11 @@
                 pltpu.VMEM(dk.shape, jnp.bfloat16),
                 pltpu.VMEM(dv.shape, jnp.bfloat16),
                 *state,
+                pltpu.VMEM((n // CHUNK, rows, CHUNK * rows), jnp.float32),
+                pltpu.VMEM((n // CHUNK, 1, CHUNK * rows), jnp.float32),
                 pltpu.SemaphoreType.DMA((4, n, PIECES)),
                 pltpu.SemaphoreType.DMA((n, PIECES)),
-                pltpu.SemaphoreType.DMA((12,)),
+                pltpu.SemaphoreType.DMA((4 * PIECES + 4,)),
             ],
             compiler_params=pltpu.CompilerParams(
                 collective_id=0, has_side_effects=True, vmem_limit_bytes=63 * 1024 * 1024

time: 30.9 us -> 29.1 us (0.942)
  Pallas kernels: 27.6 us -> 25.8 us
    pallas_call x1, Pallas kernels: 27.6 us -> 25.8 us  [body_fn(): pl.pallas_call(functools.partial(ring_kernel, n), out_shape=out_shape, in...]
where the time goes in v3:
time: 29.1 us; the launch traced here: 28.9 us
  Pallas kernels  25.8 us (89%)
  local copies, waits for them, and re-layouts  2.48 us (9%)
  between operations  0.65 us (2%)
    pallas_call x1, Pallas kernels, body_fn(): pl.pallas_call(functools.partial(ring_kernel, n), out_shape=out_shape, in...  25.8 us
    unnamed x4, local copies, waits for them, and re-layouts  2.48 us

profile of v3, /device:TPU:0, one launch (start us, length us, event | category | flops | bytes accessed | tf_op | source)
XLA Modules:
  0.0 28.9 jit_solution(11796053938715139708)
XLA Ops:
  0.6 25.8 %shard_map.113 = (bf16[64,4096]{1,0:T(8,128)(2,1)}, bf16[32,128]{1,0:T(8,128)(2,1)}) custom-call(s32[2,16]{1,0:T(2,128)} %bitcast.8, s32[2,16]{1,0:T(2,128)} %bitcast.9, bf16[64,512]{1,0:T(8,128)(2,1)} %pk.1, bf16[64,512]{1,0:T(8,128)(2,1)} %pv.1, bf16[8,512]{1,0:T(8,128)(2,1)} %ck.1, bf16[8,512]{1,0:T(8,128)(2,1)} %cv.1, bf16[64,4096]{1,0:T(8,128)(2,1)} %q_hbm.1, ...), custom_call_target="tpu_custom_call" | custom-call | tf_op jit(solution)/shard_map/pallas_call | solution.py:443
  26.5 0.0 copy-start
  26.5 1.9 %copy.14 = bf16[64,4096]{1,0:T(8,128)(2,1)} copy(bf16[64,4096]{1,0:T(8,128)(2,1)} %get-tuple-element.8) | data formatting | bytes 1048576
  28.3 0.0 copy-done
  28.3 0.6 %copy.15 = bf16[4096]{0:T(1024)(128)(2,1)} copy(bf16[4096]{0:T(1024)(128)(2,1)S(1)} %bitcast.7) | data formatting | bytes 16384
Async XLA Ops:
  26.5 1.9 %copy-start = (bf16[32,128]{1,0:T(8,128)(2,1)S(1)}, bf16[32,128]{1,0:T(8,128)(2,1)}, u32[]{:S(2)}) copy-start(bf16[32,128]{1,0:T(8,128)(2,1)} %get-tuple-element.5) | copy-start | bytes 24580

commit v4 on v3

--- a/solution.py
+++ b/solution.py
@@ -343,6 +343,9 @@
 
     inside = near == 1
     outside = near == 0
+    body.init()
+    for s in range(lines):
+        spans[s], steps[s] = body.bias(me, order[s] * CHUNK)
     for p in range(PIECES):
         from_column(order[1], p)
 
@@ -355,9 +358,6 @@
         if p == 0:
             for d in query_copies:
                 d.wait()
-            body.init()
-            for s in range(lines):
-                spans[s], steps[s] = body.bias(me, order[s] * CHUNK)
 
     @pl.when(inside)
     def _():

time: 29.1 us -> 29.1 us (level)
  no operation moved by 1% of the time
where the time goes in v4:
time: 29.1 us; the launch traced here: 28.9 us
  Pallas kernels  25.8 us (89%)
  local copies, waits for them, and re-layouts  2.48 us (9%)
  between operations  0.65 us (2%)
    pallas_call x1, Pallas kernels, body_fn(): pl.pallas_call(functools.partial(ring_kernel, n), out_shape=out_shape, in...  25.8 us
    unnamed x4, local copies, waits for them, and re-layouts  2.48 us

profile of v4, /device:TPU:0, one launch (start us, length us, event | category | flops | bytes accessed | tf_op | source)
XLA Modules:
  0.0 28.9 jit_solution(13780405558891490314)
XLA Ops:
  0.6 25.8 %shard_map.113 = (bf16[64,4096]{1,0:T(8,128)(2,1)}, bf16[32,128]{1,0:T(8,128)(2,1)}) custom-call(s32[2,16]{1,0:T(2,128)} %bitcast.8, s32[2,16]{1,0:T(2,128)} %bitcast.9, bf16[64,512]{1,0:T(8,128)(2,1)} %pk.1, bf16[64,512]{1,0:T(8,128)(2,1)} %pv.1, bf16[8,512]{1,0:T(8,128)(2,1)} %ck.1, bf16[8,512]{1,0:T(8,128)(2,1)} %cv.1, bf16[64,4096]{1,0:T(8,128)(2,1)} %q_hbm.1, ...), custom_call_target="tpu_custom_call" | custom-call | tf_op jit(solution)/shard_map/pallas_call | solution.py:443
  26.5 0.0 copy-start
  26.5 1.9 %copy.14 = bf16[64,4096]{1,0:T(8,128)(2,1)} copy(bf16[64,4096]{1,0:T(8,128)(2,1)} %get-tuple-element.8) | data formatting | bytes 1048576
  28.3 0.0 copy-done
  28.3 0.6 %copy.15 = bf16[4096]{0:T(1024)(128)(2,1)} copy(bf16[4096]{0:T(1024)(128)(2,1)S(1)} %bitcast.7) | data formatting | bytes 16384
Async XLA Ops:
  26.5 1.9 %copy-start = (bf16[32,128]{1,0:T(8,128)(2,1)S(1)}, bf16[32,128]{1,0:T(8,128)(2,1)}, u32[]{:S(2)}) copy-start(bf16[32,128]{1,0:T(8,128)(2,1)} %get-tuple-element.5) | copy-start | bytes 24580
